TPU v7x, 32 devices: a whole 2x2x4 slice. The times are simulated.
32 devices in a mesh: dp: 8 (over y, x, core), mp: 4 (over z).
Axes of the slice: x: 2, y: 2, z: 4, core: 2. Of those that a mesh axis runs over, the one named last changes fastest.
Arguments:
- tokens: bfloat16 [2048, 6144], P('dp', 'mp'), may hold values from -40 to 40
- norm_gain: float32 [6144], P('mp'), may hold values from 0.1 to 1.9
- w_qkv: bfloat16 [6144, 3, 4096], P('mp', None, 'dp'), may hold values from -0.078125 to 0.078125
- w_up: bfloat16 [6144, 12288], P('mp', 'dp'), may hold values from -0.078125 to 0.078125
- w_attn_out: bfloat16 [4096, 6144], P('dp', 'mp'), may hold values from -0.09375 to 0.09375
- w_down: bfloat16 [12288, 6144], P('dp', 'mp'), may hold values from -0.0546875 to 0.0546875
Outputs:
- layer_out: bfloat16 [2048, 6144], P('dp', 'mp')
All inputs are finite; a program needn't handle non-finite values.
Results may differ from a plain program's by a relative error of at most 0.015.
Values may be sent and summed in bfloat16 or wider, within the bound.
A program may use at most 128 MiB of HBM per device.

v0:
```python
import jax
import jax.numpy as jnp
from jax import lax
from jax.sharding import PartitionSpec as P

HEAD_DIM = 128
PATCHES = 256
EPS = 1e-06


def normalize_rows(values, total, squares, gain, width):
    mean = total / width
    spread = squares / width - mean * mean
    scaled = (values - mean[:, None]) * lax.rsqrt(spread + EPS)[:, None]
    return (scaled * gain[None, :]).astype(jnp.bfloat16)


def head_norm(values):
    mean = jnp.mean(values, axis=-1, keepdims=True)
    centered = values - mean
    spread = jnp.mean(centered * centered, axis=-1, keepdims=True)
    return centered * lax.rsqrt(spread + EPS)


def attend(qkv, heads_here):
    rows = qkv.shape[0]
    images = rows // PATCHES
    parts = qkv.reshape(images, PATCHES, 3, heads_here, HEAD_DIM)
    query = (head_norm(parts[:, :, 0].astype(jnp.float32)) * (1.0 / HEAD_DIM) ** 0.5).astype(
        jnp.bfloat16
    )
    keys = head_norm(parts[:, :, 1].astype(jnp.float32)).astype(jnp.bfloat16)
    values = parts[:, :, 2]
    scores = jnp.einsum("iqhd,ikhd->ihqk", query, keys, preferred_element_type=jnp.float32)
    weights = jnp.exp(scores)
    probs = (weights / jnp.sum(weights, axis=-1, keepdims=True)).astype(jnp.bfloat16)
    mixed = jnp.einsum("ihqk,ikhd->iqhd", probs, values, preferred_element_type=jnp.float32)
    return mixed.astype(jnp.bfloat16).reshape(rows, heads_here * HEAD_DIM)


def local(tokens, norm_gain, w_qkv, w_up, w_attn_out, w_down):
    n_mp = lax.axis_size("mp")
    feat_here = tokens.shape[1]
    head_cols = w_qkv.shape[2]
    heads_here = head_cols // HEAD_DIM
    width = feat_here * n_mp
    tokens_f = tokens.astype(jnp.float32)
    total, squares = lax.psum(
        (jnp.sum(tokens_f, axis=1), jnp.sum(tokens_f * tokens_f, axis=1)), "mp"
    )
    normed = normalize_rows(tokens_f, total, squares, norm_gain, width)
    normed_all = lax.all_gather(normed, "dp", axis=0, tiled=True)
    w_heads = w_qkv.reshape(feat_here, 3 * head_cols)
    projected = lax.psum_scatter(
        jnp.concatenate(
            [
                jnp.dot(normed_all, w_heads, preferred_element_type=jnp.float32),
                jnp.dot(normed_all, w_up, preferred_element_type=jnp.float32),
            ],
            axis=1,
        ).astype(jnp.bfloat16),
        "mp",
        scatter_dimension=0,
        tiled=True,
    )
    qkv = projected[:, : 3 * head_cols].reshape(projected.shape[0], 3, head_cols)
    attended = attend(qkv, heads_here)
    activated = jax.nn.gelu(projected[:, 3 * head_cols :].astype(jnp.float32)).astype(jnp.bfloat16)
    hidden = jnp.concatenate([attended, activated], axis=1)
    piece = lax.all_gather(hidden, "mp", axis=0, tiled=True)
    result = jnp.dot(piece[:, :head_cols], w_attn_out, preferred_element_type=jnp.float32)
    partial_out = result + jnp.dot(piece[:, head_cols:], w_down, preferred_element_type=jnp.float32)
    summed = lax.psum_scatter(
        partial_out.astype(jnp.bfloat16), "dp", scatter_dimension=0, tiled=True
    ).astype(jnp.float32)
    return (tokens_f + summed).astype(jnp.bfloat16)


def solution(mesh):
    placed = (
        P("dp", "mp"),
        P("mp"),
        P("mp", None, "dp"),
        P("mp", "dp"),
        P("dp", "mp"),
        P("dp", "mp"),
    )
    return jax.shard_map(
        local, mesh=mesh, in_specs=placed, out_specs=P("dp", "mp"), check_vma=False
    )
```

profile of v0, /device:TPU:0, one launch (start us, length us, event | category | flops | bytes accessed | tf_op | source)
XLA Modules:
  0.0 583.7 jit_solution(13878567147038606246)
XLA Ops:
  6.5 0.0 copy-start
  6.5 0.0 all-gather.3.cloned.1.call-start
  6.5 1.6 convert_reduce_fusion
  8.1 13.5 %all-reduce = (f32[256]{0:T(256)S(1)}, f32[256]{0:T(256)S(1)}) all-reduce(f32[256]{0:T(256)S(1)} %get-tuple-element.6, f32[256]{0:T(256)S(1)} %get-tuple-element.5), channel_id=1, replica_groups=mesh['dp'=8,'mp'=4] {'mp'}, use_global_device_ids=true, to_apply=%region_3.0 | all-reduce | flops 512 | bytes 4096 | tf_op jit(solution)/shard_map/psum | solution.py:48
  21.6 2.3 fusion.11
  24.0 0.0 all-gather.3.cloned.1.call-update
  24.0 0.0 reduce-scatter.3.cloned.1.call-start
  24.0 6.8 %copy.12 = bf16[1536,3,512]{0,2,1:T(8,128)(2,1)} copy(bf16[1536,3,512]{2,0,1:T(8,128)(2,1)} %param.8) | data formatting | bytes 9437184 | tf_op args[2]
  30.8 36.9 %all-gather.3.cloned.1.call-done = bf16[2048,1536]{1,0:T(8,128)(2,1)} async-done(((bf16[256,1536]{1,0:T(8,128)(2,1)}), bf16[2048,1536]{1,0:T(8,128)(2,1)}) %all-gather.3.cloned.1.call-update) | async-done | bytes 6291472 | tf_op jit(solution)/shard_map/all_gather | solution.py:52
  67.7 13.5 %convolution_convert_fusion.1 = bf16[2048,1536]{0,1:T(8,128)(2,1)S(1)} fusion(bf16[2048,1536]{1,0:T(8,128)(2,1)} %all-gather.3.cloned.1.call-done, bf16[1536,1536]{0,1:T(8,128)(2,1)} %bitcast.51), kind=kOutput, calls=%fused_computation.3 | convolution fusion | flops 9666822144 | bytes 17301504 | tf_op jit(solution)/shard_map/dot_general | solution.py:57
  81.3 13.5 %convolution_convert_fusion = bf16[2048,1536]{0,1:T(8,128)(2,1)S(1)} fusion(bf16[2048,1536]{1,0:T(8,128)(2,1)} %all-gather.3.cloned.1.call-done, bf16[1536,1536]{1,0:T(8,128)(2,1)} %param.9), kind=kOutput, calls=%fused_computation.2 | convolution fusion | flops 9666822144 | bytes 17301504 | tf_op jit(solution)/shard_map/dot_general | solution.py:58
  94.8 14.5 %pad_maximum_fusion = bf16[2048,3072]{0,1:T(8,128)(2,1)} fusion(bf16[2048,1536]{0,1:T(8,128)(2,1)S(1)} %convolution_convert_fusion, bf16[2048,1536]{0,1:T(8,128)(2,1)S(1)} %convolution_convert_fusion.1), kind=kLoop, calls=%fused_computation | loop fusion | flops 25165824 | bytes 25165824 | tf_op jit(solution)/shard_map/concatenate | solution.py:55
  109.4 0.0 reduce-scatter.3.cloned.1.call-update
  109.4 0.2 all-gather.5.cloned.1.call-start
  109.6 211.8 %reduce-scatter.3.cloned.1.call-done = bf16[512,3072]{0,1:T(8,128)(2,1)} async-done(((bf16[2048,3072]{0,1:T(8,128)(2,1)}), bf16[512,3072]{0,1:T(8,128)(2,1)}) %reduce-scatter.3.cloned.1.call-update) | async-done | bytes 3145744 | tf_op jit(solution)/shard_map/reduce_scatter | solution.py:54
  321.4 2.7 slice.28
  324.1 2.4 reshape_reshape.3
  326.4 2.2 fusion.35
  328.6 1.4 copy.21
  330.0 0.2 convert_reduce_fusion.1
  330.2 0.0 copy-start.3
  330.2 0.7 fusion.24
  330.9 1.4 copy.20
  332.2 0.2 convert_reduce_fusion.2
  332.4 0.7 fusion.18
  333.1 2.8 exponential_reduce_fusion
  335.9 0.0 copy-done.3
  336.0 0.0 copy-start.2
  336.0 0.5 fusion.14
  336.5 0.5 copy.17
  337.0 0.1 copy.22
  337.1 0.7 copy-done.2
  337.8 1.1 fusion.6
  338.9 1.5 pad_maximum_fusion.1
  340.4 0.0 all-gather.5.cloned.1.call-update
  340.4 0.0 reduce-scatter.5.cloned.1.call-start
  340.5 150.8 %all-gather.5.cloned.1.call-done = bf16[2048,2048]{0,1:T(8,128)(2,1)} async-done(((bf16[512,2048]{0,1:T(8,128)(2,1)}), bf16[2048,2048]{0,1:T(8,128)(2,1)}) %all-gather.5.cloned.1.call-update) | async-done | bytes 8388624 | tf_op jit(solution)/shard_map/all_gather | solution.py:70
  491.3 0.0 copy-done
  491.3 0.0 copy-start.4
  491.3 8.2 %fusion.7 = f32[2048,1536]{1,0:T(8,128)} fusion(bf16[512,1536]{1,0:T(8,128)(2,1)S(1)} %copy-done, bf16[2048,2048]{0,1:T(8,128)(2,1)} %all-gather.5.cloned.1.call-done), kind=kOutput, calls=%fused_computation.19 | convolution fusion | flops 3221225472 | bytes 16252928 | tf_op jit(solution)/shard_map/dot_general | solution.py:71
  499.5 0.0 copy-done.4
  499.5 15.3 %add_convert_fusion = bf16[2048,1536]{1,0:T(8,128)(2,1)} fusion(f32[2048,1536]{1,0:T(8,128)} %fusion.7, bf16[1536,1536]{1,0:T(8,128)(2,1)} %param.11, bf16[2048,2048]{0,1:T(8,128)(2,1)S(1)} %copy-done.4), kind=kOutput, calls=%fused_computation.1 | convolution fusion | flops 9669967872 | bytes 29884416 | tf_op jit(solution)/shard_map/dot_general | solution.py:72
  514.8 0.0 copy-start.1
  514.8 0.0 reduce-scatter.5.cloned.1.call-update
  514.9 60.1 %reduce-scatter.5.cloned.1.call-done = bf16[256,1536]{1,0:T(8,128)(2,1)} async-done(((bf16[2048,1536]{1,0:T(8,128)(2,1)}), bf16[256,1536]{1,0:T(8,128)(2,1)}) %reduce-scatter.5.cloned.1.call-update) | async-done | bytes 786448 | tf_op jit(solution)/shard_map/reduce_scatter | solution.py:73
  575.0 0.0 copy-done.1
  575.0 2.2 fusion.13
  (4 shorter events, 0.0 us)
Async XLA Ops:
  6.5 484.7 %copy-start = (bf16[512,1536]{1,0:T(8,128)(2,1)S(1)}, bf16[512,1536]{1,0:T(8,128)(2,1)}, u32[]{:S(2)}) copy-start(bf16[512,1536]{1,0:T(8,128)(2,1)} %param.10) | copy-start | bytes 4718596
  6.5 61.2 %all-gather.3.cloned.1.call-start = ((), (), s32[]{:S(2)}) async-start(), calls=%async_computation.2 | async-start | bytes 7077888 | tf_op jit(solution)/shard_map/all_gather | solution.py:52
  24.0 297.4 %reduce-scatter.3.cloned.1.call-start = ((), (), s32[]{:S(2)}) async-start(), calls=%async_computation.3 | async-start | bytes 15728640 | tf_op jit(solution)/shard_map/reduce_scatter | solution.py:54
  109.4 381.9 %all-gather.5.cloned.1.call-start = ((), (), s32[]{:S(2)}) async-start(), calls=%async_computation.4 | async-start | bytes 10485760 | tf_op jit(solution)/shard_map/all_gather | solution.py:70
  330.2 5.8 copy-start.3
  336.0 1.9 copy-start.2
  340.4 234.5 %reduce-scatter.5.cloned.1.call-start = ((), (), s32[]{:S(2)}) async-start(), calls=%async_computation.5 | async-start | bytes 7077888 | tf_op jit(solution)/shard_map/reduce_scatter | solution.py:73
  491.3 8.2 %copy-start.4 = (bf16[2048,2048]{0,1:T(8,128)(2,1)S(1)}, bf16[2048,2048]{0,1:T(8,128)(2,1)}, u32[]{:S(2)}) copy-start(bf16[2048,2048]{0,1:T(8,128)(2,1)} %all-gather.5.cloned.1.call-done) | copy-start | bytes 25165828
  514.8 60.1 %copy-start.1 = (bf16[256,1536]{1,0:T(8,128)(2,1)S(1)}, bf16[256,1536]{1,0:T(8,128)(2,1)}, u32[]{:S(2)}) copy-start(bf16[256,1536]{1,0:T(8,128)(2,1)} %param.6) | copy-start | bytes 2359300
Sparse Core Ops, SparseCore 0:
  24.1 43.5 all-gather.2
  109.5 211.8 reduce-scatter.2
  340.6 150.6 all-gather.4
  515.0 59.9 reduce-scatter.4
where the time goes:
time: 584 us
  waiting for transfers between devices  460 us (79%)
  matrix products  53.9 us (9%)
  other arithmetic  25 us (4%)
  local copies, waits for them, and re-layouts  18 us (3%)
  blocking collectives  13.5 us (2%)
  between operations  13.3 us (2%)
    reduce_scatter x1, waiting for transfers between devices, local(): lax.psum_scatter(jnp.concatenate([jnp.dot(normed_all, w_heads, preferred_...  212 us
    all_gather x1, waiting for transfers between devices, local(): piece = lax.all_gather(hidden, 'mp', axis=0, tiled=True)  151 us
    reduce_scatter x1, waiting for transfers between devices, local(): lax.psum_scatter(partial_out.astype(jnp.bfloat16), 'dp', scatter_dimensio...  60.1 us
    all_gather x1, waiting for transfers between devices, local(): normed_all = lax.all_gather(normed, 'dp', axis=0, tiled=True)  36.9 us
    dot_general x1, matrix products, local(): jnp.dot(piece[:, head_cols:], w_down, preferred_element_type=jnp.float32)  15.3 us
    concatenate x1, other arithmetic, local(): jnp.concatenate([jnp.dot(normed_all, w_heads, preferred_element_type=jnp....  14.5 us
    dot_general x1, matrix products, local(): jnp.dot(normed_all, w_heads, preferred_element_type=jnp.float32)  13.5 us
    dot_general x1, matrix products, local(): jnp.dot(normed_all, w_up, preferred_element_type=jnp.float32)  13.5 us
  transfers between devices with their start and end apart: 4, of which 4 were waited for; matrix products, arithmetic and copies ran while one was open for 1% of the time, Pallas kernels for 0%

commit v1 on v0

--- a/solution.py
+++ b/solution.py
@@ -49,7 +49,12 @@
         (jnp.sum(tokens_f, axis=1), jnp.sum(tokens_f * tokens_f, axis=1)), "mp"
     )
     normed = normalize_rows(tokens_f, total, squares, norm_gain, width)
-    normed_all = lax.all_gather(normed, "dp", axis=0, tiled=True)
+    ring = [normed]
+    for hop in range(7):
+        ring.append(lax.ppermute(ring[-1], "dp", [(dev, (dev + 1) % 8) for dev in range(8)]))
+    normed_all = jnp.roll(
+        jnp.concatenate(ring[::-1], axis=0), (lax.axis_index("dp") + 1) * ring[0].shape[0], axis=0
+    )
     w_heads = w_qkv.reshape(feat_here, 3 * head_cols)
     projected = lax.psum_scatter(
         jnp.concatenate(

time: 584 us -> 640 us (1.096)
  waiting for transfers between devices: 460 us -> 500 us
  local copies, waits for them, and re-layouts: 18 us -> 34 us
    ppermute x0 -> x7, waiting for transfers between devices: none -> 79.9 us  [local(): lax.ppermute(ring[-1], 'dp', [(dev, (dev + 1) % 8) for dev in range(8)])]
    all_gather x1 -> x0, waiting for transfers between devices: 36.9 us -> none  [local(): normed_all = lax.all_gather(normed, 'dp', axis=0, tiled=True)]
    unnamed x14 -> x50, local copies, waits for them, and re-layouts: 10.3 us -> 23.6 us
  transfers between devices with their start and end apart: 4 -> 10, of which waited for: 4 -> 10; matrix products, arithmetic and copies ran while one was open for 1% -> 1% of each run, Pallas kernels for 0% -> 0%
where the time goes in v1:
time: 640 us
  waiting for transfers between devices  500 us (78%)
  matrix products  53.6 us (8%)
  local copies, waits for them, and re-layouts  34 us (5%)
  other arithmetic  24.9 us (4%)
  blocking collectives  13.5 us (2%)
  between operations  13.4 us (2%)
    reduce_scatter x1, waiting for transfers between devices, local(): lax.psum_scatter(jnp.concatenate([jnp.dot(normed_all, w_heads, preferred_...  209 us
    all_gather x1, waiting for transfers between devices, local(): piece = lax.all_gather(hidden, 'mp', axis=0, tiled=True)  151 us
    ppermute x7, waiting for transfers between devices, local(): lax.ppermute(ring[-1], 'dp', [(dev, (dev + 1) % 8) for dev in range(8)])  79.9 us
    reduce_scatter x1, waiting for transfers between devices, local(): lax.psum_scatter(partial_out.astype(jnp.bfloat16), 'dp', scatter_dimensio...  60.1 us
    unnamed x50, local copies, waits for them, and re-layouts  23.6 us
    dot_general x1, matrix products, local(): jnp.dot(piece[:, head_cols:], w_down, preferred_element_type=jnp.float32)  15.3 us
    concatenate x1, other arithmetic, local(): jnp.concatenate([jnp.dot(normed_all, w_heads, preferred_element_type=jnp....  14.8 us
    dot_general x1, matrix products, local(): jnp.dot(normed_all, w_up, preferred_element_type=jnp.float32)  13.5 us
  transfers between devices with their start and end apart: 10, of which 10 were waited for; matrix products, arithmetic and copies ran while one was open for 1% of the time, Pallas kernels for 0%

profile of v1, /device:TPU:0, one launch (start us, length us, event | category | flops | bytes accessed | tf_op | source)
XLA Modules:
  0.0 639.8 jit_solution(10740868780414307128)
XLA Ops:
  6.5 1.6 convert_reduce_fusion
  8.1 13.5 %all-reduce = (f32[256]{0:T(256)S(1)}, f32[256]{0:T(256)S(1)}) all-reduce(f32[256]{0:T(256)S(1)} %get-tuple-element.6, f32[256]{0:T(256)S(1)} %get-tuple-element.5), channel_id=1, replica_groups=mesh['dp'=8,'mp'=4] {'mp'}, use_global_device_ids=true, to_apply=%region_3.0 | all-reduce | flops 512 | bytes 4096 | tf_op jit(solution)/shard_map/psum | solution.py:48
  21.6 1.4 fusion.13
  23.1 0.1 collective-permute-start
  23.2 12.3 %collective-permute-done = bf16[256,1536]{1,0:T(8,128)(2,1)S(1)} collective-permute-done((bf16[256,1536]{1,0:T(8,128)(2,1)S(1)}, bf16[256,1536]{1,0:T(8,128)(2,1)S(1)}, u32[]{:S(2)}, u32[]{:S(2)}) %collective-permute-start) | collective-permute-done | bytes 786464 | tf_op jit(solution)/shard_map/ppermute | solution.py:54
  35.5 12.3 %collective-permute-done.1 = bf16[256,1536]{1,0:T(8,128)(2,1)S(1)} collective-permute-done((bf16[256,1536]{1,0:T(8,128)(2,1)S(1)}, bf16[256,1536]{1,0:T(8,128)(2,1)S(1)}, u32[]{:S(2)}, u32[]{:S(2)}) %collective-permute-start.1) | collective-permute-done | bytes 786464 | tf_op jit(solution)/shard_map/ppermute | solution.py:54
  47.8 12.3 %collective-permute-done.2 = bf16[256,1536]{1,0:T(8,128)(2,1)S(1)} collective-permute-done((bf16[256,1536]{1,0:T(8,128)(2,1)S(1)}, bf16[256,1536]{1,0:T(8,128)(2,1)S(1)}, u32[]{:S(2)}, u32[]{:S(2)}) %collective-permute-start.2) | collective-permute-done | bytes 786464 | tf_op jit(solution)/shard_map/ppermute | solution.py:54
  60.1 0.9 copy-done.5
  61.0 12.3 %collective-permute-done.3 = bf16[256,1536]{1,0:T(8,128)(2,1)S(1)} collective-permute-done((bf16[256,1536]{1,0:T(8,128)(2,1)S(1)}, bf16[256,1536]{1,0:T(8,128)(2,1)S(1)}, u32[]{:S(2)}, u32[]{:S(2)}) %collective-permute-start.3) | collective-permute-done | bytes 786464 | tf_op jit(solution)/shard_map/ppermute | solution.py:54
  73.3 0.9 copy-done.7
  74.2 12.3 %collective-permute-done.4 = bf16[256,1536]{1,0:T(8,128)(2,1)S(1)} collective-permute-done((bf16[256,1536]{1,0:T(8,128)(2,1)S(1)}, bf16[256,1536]{1,0:T(8,128)(2,1)S(1)}, u32[]{:S(2)}, u32[]{:S(2)}) %collective-permute-start.4) | collective-permute-done | bytes 786464 | tf_op jit(solution)/shard_map/ppermute | solution.py:54
  86.5 0.9 copy-done.9
  87.4 12.4 %collective-permute-done.5 = bf16[256,1536]{1,0:T(8,128)(2,1)} collective-permute-done((bf16[256,1536]{1,0:T(8,128)(2,1)S(1)}, bf16[256,1536]{1,0:T(8,128)(2,1)}, u32[]{:S(2)}, u32[]{:S(2)}) %collective-permute-start.5) | collective-permute-done | bytes 786464 | tf_op jit(solution)/shard_map/ppermute | solution.py:54
  99.8 6.6 %copy.12 = bf16[1536,3,512]{0,2,1:T(8,128)(2,1)} copy(bf16[1536,3,512]{2,0,1:T(8,128)(2,1)} %param.8) | data formatting | bytes 9437184 | tf_op args[2]
  106.4 6.0 collective-permute-done.6
  112.4 1.2 constant_dynamic-update-slice_fusion.15
  113.6 1.2 constant_dynamic-update-slice_fusion.14
  114.8 1.3 constant_dynamic-update-slice_fusion.13
  116.1 1.3 constant_dynamic-update-slice_fusion.12
  117.6 0.3 constant_dynamic-update-slice_fusion.8
  117.9 1.3 constant_dynamic-update-slice_fusion.7
  119.2 1.2 constant_dynamic-update-slice_fusion.6
  120.8 0.3 constant_dynamic-update-slice_fusion
  121.1 4.5 copy-done.12
  125.6 12.1 %convolution_convert_fusion.1 = bf16[2048,1536]{0,1:T(8,128)(2,1)S(1)} fusion(bf16[1536,1536]{0,1:T(8,128)(2,1)S(1)} %bitcast.51, bf16[4096,1536]{1,0:T(8,128)(2,1)} %copy-done.12, s32[]{:T(128)S(6)} %select_n.14), kind=kOutput, calls=%fused_computation.3 | convolution fusion | flops 9666822144 | bytes 17301508 | tf_op jit(solution)/shard_map/dot_general | solution.py:62
  137.7 13.5 %convolution_convert_fusion = bf16[2048,1536]{0,1:T(8,128)(2,1)S(1)} fusion(bf16[1536,1536]{1,0:T(8,128)(2,1)} %param.9, bf16[4096,1536]{1,0:T(8,128)(2,1)} %copy-done.12, s32[]{:T(128)S(6)} %select_n.14), kind=kOutput, calls=%fused_computation.2 | convolution fusion | flops 9666822144 | bytes 17301508 | tf_op jit(solution)/shard_map/dot_general | solution.py:63
  151.3 14.8 %pad_maximum_fusion = bf16[2048,3072]{0,1:T(8,128)(2,1)} fusion(bf16[2048,1536]{0,1:T(8,128)(2,1)S(1)} %convolution_convert_fusion, bf16[2048,1536]{0,1:T(8,128)(2,1)S(1)} %convolution_convert_fusion.1), kind=kLoop, calls=%fused_computation | loop fusion | flops 25165824 | bytes 25165824 | tf_op jit(solution)/shard_map/concatenate | solution.py:60
  166.1 209.3 %reduce-scatter.3.cloned.1.call-done = bf16[512,3072]{0,1:T(8,128)(2,1)} async-done(((bf16[2048,3072]{0,1:T(8,128)(2,1)}), bf16[512,3072]{0,1:T(8,128)(2,1)}) %reduce-scatter.3.cloned.1.call-update) | async-done | bytes 3145744 | tf_op jit(solution)/shard_map/reduce_scatter | solution.py:59
  375.4 2.7 slice.28
  378.0 3.5 reshape_reshape.3
  381.6 3.6 fusion.39
  385.2 0.5 copy.20
  385.7 0.2 convert_reduce_fusion.2
  385.9 0.7 fusion.20
  386.6 1.4 copy.21
  387.9 0.2 convert_reduce_fusion.1
  388.2 0.7 fusion.26
  388.9 2.8 exponential_reduce_fusion
  391.7 1.6 fusion.16
  393.2 0.5 copy.17
  393.8 0.1 copy.22
  393.9 1.1 fusion.8
  395.0 1.5 pad_maximum_fusion.1
  396.5 150.8 %all-gather.2.cloned.1.call-done = bf16[2048,2048]{0,1:T(8,128)(2,1)} async-done(((bf16[512,2048]{0,1:T(8,128)(2,1)}), bf16[2048,2048]{0,1:T(8,128)(2,1)}) %all-gather.2.cloned.1.call-update) | async-done | bytes 8388624 | tf_op jit(solution)/shard_map/all_gather | solution.py:75
  547.3 8.3 %fusion.9 = f32[2048,1536]{1,0:T(8,128)} fusion(bf16[512,1536]{1,0:T(8,128)(2,1)S(1)} %copy-done, bf16[2048,2048]{0,1:T(8,128)(2,1)} %all-gather.2.cloned.1.call-done), kind=kOutput, calls=%fused_computation.21 | convolution fusion | flops 3221225472 | bytes 16252928 | tf_op jit(solution)/shard_map/dot_general | solution.py:76
  555.6 15.3 %add_convert_fusion = bf16[2048,1536]{1,0:T(8,128)(2,1)} fusion(f32[2048,1536]{1,0:T(8,128)} %fusion.9, bf16[1536,1536]{1,0:T(8,128)(2,1)} %param.11, bf16[2048,2048]{0,1:T(8,128)(2,1)S(1)} %copy-done.13), kind=kOutput, calls=%fused_computation.1 | convolution fusion | flops 9669967872 | bytes 29884416 | tf_op jit(solution)/shard_map/dot_general | solution.py:77
  570.9 60.1 %reduce-scatter.5.cloned.1.call-done = bf16[256,1536]{1,0:T(8,128)(2,1)} async-done(((bf16[2048,1536]{1,0:T(8,128)(2,1)}), bf16[256,1536]{1,0:T(8,128)(2,1)}) %reduce-scatter.5.cloned.1.call-update) | async-done | bytes 786448 | tf_op jit(solution)/shard_map/reduce_scatter | solution.py:78
  631.0 2.2 fusion.15
  (53 shorter events, 0.7 us)
Async XLA Ops:
  6.5 540.7 %copy-start = (bf16[512,1536]{1,0:T(8,128)(2,1)S(1)}, bf16[512,1536]{1,0:T(8,128)(2,1)}, u32[]{:S(2)}) copy-start(bf16[512,1536]{1,0:T(8,128)(2,1)} %param.10) | copy-start | bytes 4718596
  6.5 368.8 %reduce-scatter.3.cloned.1.call-start = ((), (), s32[]{:S(2)}) async-start(), calls=%async_computation.2 | async-start | bytes 15728640 | tf_op jit(solution)/shard_map/reduce_scatter | solution.py:59
  23.1 12.4 %collective-permute-start = (bf16[256,1536]{1,0:T(8,128)(2,1)S(1)}, bf16[256,1536]{1,0:T(8,128)(2,1)S(1)}, u32[]{:S(2)}, u32[]{:S(2)}) collective-permute-start(bf16[256,1536]{1,0:T(8,128)(2,1)S(1)} %fusion.13), channel_id=1, source_target_pairs={{0,4},{4,8},{8,12},{12,16},{16,20},{20,24},{24,28},{28,0},{1,5},{5... | collective-permute-start | bytes 2359304 | tf_op jit(solution)/shard_map/ppermute | solution.py:54
  35.5 12.3 %collective-permute-start.1 = (bf16[256,1536]{1,0:T(8,128)(2,1)S(1)}, bf16[256,1536]{1,0:T(8,128)(2,1)S(1)}, u32[]{:S(2)}, u32[]{:S(2)}) collective-permute-start(bf16[256,1536]{1,0:T(8,128)(2,1)S(1)} %collective-permute-done), channel_id=1, source_target_pairs={{0,4},{4,8},{8,12},{12,16},{16,20},{20,24},{24,28},{28,0},{1,5},{5... | collective-permute-start | bytes 2359304 | tf_op jit(solution)/shard_map/ppermute | solution.py:54
  47.8 52.0 %copy-start.3 = (bf16[256,1536]{1,0:T(8,128)(2,1)}, bf16[256,1536]{1,0:T(8,128)(2,1)S(1)}, u32[]{:S(2)}) copy-start(bf16[256,1536]{1,0:T(8,128)(2,1)S(1)} %collective-permute-done.1) | copy-start | bytes 2359300
  47.8 12.3 %collective-permute-start.2 = (bf16[256,1536]{1,0:T(8,128)(2,1)S(1)}, bf16[256,1536]{1,0:T(8,128)(2,1)S(1)}, u32[]{:S(2)}, u32[]{:S(2)}) collective-permute-start(bf16[256,1536]{1,0:T(8,128)(2,1)S(1)} %collective-permute-done.1), channel_id=1, source_target_pairs={{0,4},{4,8},{8,12},{12,16},{16,20},{20,24},{24,28},{28,0},{1,5},{5... | collective-permute-start | bytes 2359304 | tf_op jit(solution)/shard_map/ppermute | solution.py:54
  60.1 0.9 copy-start.5
  61.0 12.3 %collective-permute-start.3 = (bf16[256,1536]{1,0:T(8,128)(2,1)S(1)}, bf16[256,1536]{1,0:T(8,128)(2,1)S(1)}, u32[]{:S(2)}, u32[]{:S(2)}) collective-permute-start(bf16[256,1536]{1,0:T(8,128)(2,1)S(1)} %collective-permute-done.2), channel_id=1, source_target_pairs={{0,4},{4,8},{8,12},{12,16},{16,20},{20,24},{24,28},{28,0},{1,5},{5... | collective-permute-start | bytes 2359304 | tf_op jit(solution)/shard_map/ppermute | solution.py:54
  73.3 0.9 copy-start.7
  74.2 12.3 %collective-permute-start.4 = (bf16[256,1536]{1,0:T(8,128)(2,1)S(1)}, bf16[256,1536]{1,0:T(8,128)(2,1)S(1)}, u32[]{:S(2)}, u32[]{:S(2)}) collective-permute-start(bf16[256,1536]{1,0:T(8,128)(2,1)S(1)} %collective-permute-done.3), channel_id=1, source_target_pairs={{0,4},{4,8},{8,12},{12,16},{16,20},{20,24},{24,28},{28,0},{1,5},{5... | collective-permute-start | bytes 2359304 | tf_op jit(solution)/shard_map/ppermute | solution.py:54
  86.5 0.9 copy-start.9
  87.4 12.4 %collective-permute-start.5 = (bf16[256,1536]{1,0:T(8,128)(2,1)S(1)}, bf16[256,1536]{1,0:T(8,128)(2,1)}, u32[]{:S(2)}, u32[]{:S(2)}) collective-permute-start(bf16[256,1536]{1,0:T(8,128)(2,1)S(1)} %collective-permute-done.4), channel_id=1, source_target_pairs={{0,4},{4,8},{8,12},{12,16},{16,20},{20,24},{24,28},{28,0},{1,5},{5... | collective-permute-start | bytes 2359304 | tf_op jit(solution)/shard_map/ppermute | solution.py:54
  99.8 12.6 %collective-permute-start.6 = (bf16[256,1536]{1,0:T(8,128)(2,1)}, bf16[256,1536]{1,0:T(8,128)(2,1)}, u32[]{:S(2)}, u32[]{:S(2)}) collective-permute-start(bf16[256,1536]{1,0:T(8,128)(2,1)} %collective-permute-done.5), channel_id=1, source_target_pairs={{0,4},{4,8},{8,12},{12,16},{16,20},{20,24},{24,28},{28,0},{1,5},{5... | collective-permute-start | bytes 2359304 | tf_op jit(solution)/shard_map/ppermute | solution.py:54
  106.4 11.1 %copy-start.1 = (bf16[256,1536]{1,0:T(8,128)(2,1)S(1)}, bf16[256,1536]{1,0:T(8,128)(2,1)}, u32[]{:S(2)}) copy-start(bf16[256,1536]{1,0:T(8,128)(2,1)} %param.6) | copy-start | bytes 2359300
  106.4 11.1 %copy-start.11 = (f32[1536]{0:T(1024)S(1)}, f32[1536]{0:T(1024)}, u32[]{:S(2)}) copy-start(f32[1536]{0:T(1024)} %param.7) | copy-start | bytes 18436
  106.4 10.9 %copy-start.6 = (bf16[256,1536]{1,0:T(8,128)(2,1)S(1)}, bf16[256,1536]{1,0:T(8,128)(2,1)}, u32[]{:S(2)}) copy-start(bf16[256,1536]{1,0:T(8,128)(2,1)} %copy-done.5) | copy-start | bytes 2359300
  106.4 11.0 %copy-start.4 = (bf16[256,1536]{1,0:T(8,128)(2,1)S(1)}, bf16[256,1536]{1,0:T(8,128)(2,1)}, u32[]{:S(2)}) copy-start(bf16[256,1536]{1,0:T(8,128)(2,1)} %copy-done.3) | copy-start | bytes 2359300
  114.8 5.6 copy-start.10
  116.1 4.4 copy-start.8
  117.6 8.0 %slice-start = ((s8[4718592]{0:T(1024)(128)(4,1)}), s8[4194304]{0:T(1024)(128)(4,1)S(1)}, s32[]{:S(2)}) async-start(s8[4718592]{0:T(1024)(128)(4,1)} %bitcast.49), calls=%async_computation.5 | async-start | bytes 8388608
  120.5 5.1 slice-start.1
  121.1 4.5 copy-start.12
  166.1 381.2 %all-gather.2.cloned.1.call-start = ((), (), s32[]{:S(2)}) async-start(), calls=%async_computation.3 | async-start | bytes 10485760 | tf_op jit(solution)/shard_map/all_gather | solution.py:75
  388.8 5.0 copy-start.2
  396.5 234.6 %reduce-scatter.5.cloned.1.call-start = ((), (), s32[]{:S(2)}) async-start(), calls=%async_computation.4 | async-start | bytes 7077888 | tf_op jit(solution)/shard_map/reduce_scatter | solution.py:78
  547.3 8.3 %copy-start.13 = (bf16[2048,2048]{0,1:T(8,128)(2,1)S(1)}, bf16[2048,2048]{0,1:T(8,128)(2,1)}, u32[]{:S(2)}) copy-start(bf16[2048,2048]{0,1:T(8,128)(2,1)} %all-gather.2.cloned.1.call-done) | copy-start | bytes 25165828
Sparse Core Ops, SparseCore 0:
  166.2 209.1 reduce-scatter.2
  396.6 150.6 all-gather.1
  571.1 59.9 reduce-scatter.4
